TPU v7x, 32 devices: a whole 2x2x4 slice. The times are simulated.
32 devices in a mesh: clip: 4 (over x, core), tx: 4 (over z), ty: 2 (over y).
Axes of the slice: x: 2, y: 2, z: 4, core: 2. Of those that a mesh axis runs over, the one named last changes fastest.
Arguments:
- query_states: bfloat16 [32, 128, 1152], P(('clip', 'tx', 'ty')), parts along dimension 0, may hold values from -64 to 64
- key_states: bfloat16 [32, 128, 1152], P(('clip', 'tx', 'ty')), parts along dimension 0, may hold values from -24 to 24
- value_states: bfloat16 [32, 128, 1152], P(('clip', 'tx', 'ty')), parts along dimension 0, may hold values from -6 to 6
- grad_output: bfloat16 [32, 128, 1152], P(('clip', 'tx', 'ty')), parts along dimension 0, may hold values from -6 to 6
- branch_gate: float32 [4608], P('clip'), parts along dimension 0, may hold values from 0.1 to 1.9
- out_weight: bfloat16 [1152, 1152], P('tx'), may hold values from -0.1875 to 0.1875
Outputs:
- query_grad: bfloat16 [32, 128, 1152], P(('clip', 'tx', 'ty')), parts along dimension 0
- key_grad: bfloat16 [32, 128, 1152], P(('clip', 'tx', 'ty')), parts along dimension 0
- value_grad: bfloat16 [32, 128, 1152], P(('clip', 'tx', 'ty')), parts along dimension 0
- gate_grad: float32 [4608], P('clip'), parts along dimension 0
There are 4 independent parts, one for each index of `clip`. A program takes and returns all parts, laid end to end along the dimension named above; an argument that names none is the same for every part. Nothing has to cross between parts.
All inputs are finite; a program needn't handle non-finite values.
Results may differ from a plain program's by a relative error of at most 0.025.
Values may be sent and summed in bfloat16 or wider, within the bound.
A program may use at most 64 MiB of HBM per device.

v0:
```python
import jax
import jax.numpy as jnp
from jax import lax
from jax.sharding import PartitionSpec as P

HEAD_DIM = 72


def shortened(x):

    def short(part):
        return part.astype(jnp.bfloat16) if part.dtype == jnp.float32 else part

    return jax.tree.map(short, x)


def attend_block(queries, keys_in, values_in, grads_in):
    frames, block_pos, block_width = queries.shape
    heads_here = block_width // HEAD_DIM
    shape4 = (frames, block_pos, heads_here, HEAD_DIM)
    q_four = queries.reshape(shape4)
    k_four = keys_in.reshape(shape4)
    v_four = values_in.reshape(shape4)
    g_four = grads_in.reshape(shape4)
    factor = HEAD_DIM ** (-0.5)
    scores = (
        jnp.einsum("fphd,gphd->phfg", q_four, k_four, preferred_element_type=jnp.float32) * factor
    )
    peak = jnp.max(scores, axis=-1, keepdims=True)
    expon = jnp.exp(scores - peak)
    probs = expon / jnp.sum(expon, axis=-1, keepdims=True)
    probs_b = probs.astype(jnp.bfloat16)
    attn_out = jnp.einsum(
        "phfg,gphd->fphd", probs_b, v_four, preferred_element_type=jnp.float32
    ).astype(jnp.bfloat16)
    value_grad = jnp.einsum(
        "phfg,fphd->gphd", probs_b, g_four, preferred_element_type=jnp.float32
    ).astype(jnp.bfloat16)
    dprobs = jnp.einsum("fphd,gphd->phfg", g_four, v_four, preferred_element_type=jnp.float32)
    delta = jnp.sum(g_four.astype(jnp.float32) * attn_out.astype(jnp.float32), axis=-1)
    delta = jnp.transpose(delta, (1, 2, 0))[..., None]
    dscores = (probs * (dprobs - delta) * factor).astype(jnp.bfloat16)
    query_grad = jnp.einsum(
        "phfg,gphd->fphd", dscores, k_four, preferred_element_type=jnp.float32
    ).astype(jnp.bfloat16)
    key_grad = jnp.einsum(
        "phfg,fphd->gphd", dscores, q_four, preferred_element_type=jnp.float32
    ).astype(jnp.bfloat16)
    flat = (frames, block_pos, block_width)
    return (
        query_grad.reshape(flat),
        key_grad.reshape(flat),
        value_grad.reshape(flat),
        attn_out.reshape(flat),
    )


def split_for_direct(array, across_x, across_y):
    positions, width = array.shape
    pieces = array.reshape(across_y, positions // across_y, across_x, width // across_x)
    pieces = jnp.transpose(pieces, (2, 0, 1, 3))
    return pieces.reshape(1, across_x * across_y, positions // across_y, width // across_x)


def join_from_direct(array, across_x, across_y):
    block_pos, block_width = (array.shape[2], array.shape[3])
    pieces = array.reshape(across_x, across_y, block_pos, block_width)
    pieces = jnp.transpose(pieces, (1, 2, 0, 3))
    return pieces.reshape(1, across_y * block_pos, across_x * block_width)


def per_device(query_states, key_states, value_states, grad_output, branch_gate, out_weight):
    across_x = lax.axis_size("tx")
    across_y = lax.axis_size("ty")
    devices_here = across_x * across_y
    positions = grad_output.shape[1]
    width = grad_output.shape[2]
    block_pos = positions // across_y
    block_width = width // across_x
    grad_rows = grad_output[0]
    gated = (grad_rows.astype(jnp.float32) * branch_gate).astype(jnp.bfloat16)
    d_attn = lax.dot_general(
        gated,
        lax.all_gather(out_weight, "tx", axis=0, tiled=True),
        (((1,), (1,)), ((), ())),
        preferred_element_type=jnp.float32,
    )
    d_attn = d_attn.astype(jnp.bfloat16)
    sources = (query_states[0], key_states[0], value_states[0], d_attn)
    prepared = tuple((split_for_direct(arr, across_x, across_y) for arr in sources))
    moved = jax.tree.map(
        lambda part, own: part.astype(own.dtype),
        lax.all_to_all(shortened(prepared), ("tx", "ty"), split_axis=1, concat_axis=0, tiled=True),
        prepared,
    )
    moved = tuple((arr.reshape(devices_here, block_pos, block_width) for arr in moved))
    results = attend_block(moved[0], moved[1], moved[2], moved[3])
    outgoing = tuple((arr.reshape(devices_here, 1, block_pos, block_width) for arr in results))
    returned = jax.tree.map(
        lambda part, own: part.astype(own.dtype),
        lax.all_to_all(shortened(outgoing), ("tx", "ty"), split_axis=0, concat_axis=1, tiled=True),
        outgoing,
    )
    returned = tuple((join_from_direct(arr, across_x, across_y) for arr in returned))
    query_grad, key_grad, value_grad, attn_frame = returned
    attn_rows = attn_frame[0]
    branch_out = jnp.dot(
        attn_rows,
        lax.all_gather(out_weight, "tx", axis=0, tiled=True),
        preferred_element_type=jnp.float32,
    )
    local_terms = jnp.sum(grad_rows.astype(jnp.float32) * branch_out, axis=0)
    gate_grad = lax.psum(local_terms, ("tx", "ty"))
    return (query_grad, key_grad, value_grad, gate_grad)


def solution(mesh):
    in_specs = (
        P(("clip", "tx", "ty"), None, None),
        P(("clip", "tx", "ty"), None, None),
        P(("clip", "tx", "ty"), None, None),
        P(("clip", "tx", "ty"), None, None),
        P("clip"),
        P("tx", None),
    )
    out_specs = (
        P(("clip", "tx", "ty"), None, None),
        P(("clip", "tx", "ty"), None, None),
        P(("clip", "tx", "ty"), None, None),
        P("clip"),
    )
    return jax.shard_map(
        per_device, mesh=mesh, in_specs=in_specs, out_specs=out_specs, check_vma=False
    )
```

profile of v0, /device:TPU:0, one launch (start us, length us, event | category | flops | bytes accessed | tf_op | source)
XLA Modules:
  0.0 204.5 jit_solution(13158037343326057094)
XLA Ops:
  7.2 0.0 copy-start.3
  7.2 0.0 copy-start.4
  7.2 0.0 all-gather.2.cloned.1.call-start
  7.2 0.7 all-gather.2.cloned.1.call-update
  7.9 1.3 reshape_squeeze.9
  9.2 0.8 copy.55
  10.1 7.4 %all-to-all-start = ((bf16[1,8,64,288]{3,2,0,1:T(8,128)(2,1)}), bf16[1,8,64,288]{3,2,0,1:T(8,128)(2,1)S(1)}, u32[]{:S(2)}, u32[]{:S(2)}) async-start(bf16[1,8,64,288]{3,2,0,1:T(8,128)(2,1)} %bitcast.2), calls=%async_computation | async-start | bytes 786432 | tf_op jit(solution)/shard_map/all_to_all | solution.py:93
  17.5 0.0 copy-done.3
  17.5 0.4 reshape_squeeze.10
  17.9 0.8 copy.57
  18.7 19.1 %all-to-all-done = bf16[1,8,64,288]{3,2,0,1:T(8,128)(2,1)S(1)} async-done(((bf16[1,8,64,288]{3,2,0,1:T(8,128)(2,1)}), bf16[1,8,64,288]{3,2,0,1:T(8,128)(2,1)S(1)}, u32[]{:S(2)}, u32[]{:S(2)}) %all-to-all-start) | async-done | bytes 294944 | tf_op jit(solution)/shard_map/all_to_all | solution.py:93
  37.8 6.1 %all-to-all-start.1 = ((bf16[1,8,64,288]{3,2,0,1:T(8,128)(2,1)}), bf16[1,8,64,288]{3,2,0,1:T(8,128)(2,1)S(1)}, u32[]{:S(2)}, u32[]{:S(2)}) async-start(bf16[1,8,64,288]{3,2,0,1:T(8,128)(2,1)} %bitcast.5), calls=%async_computation.1 | async-start | bytes 786432 | tf_op jit(solution)/shard_map/all_to_all | solution.py:93
  43.8 0.0 copy-done.4
  43.8 0.4 reshape_squeeze.11
  44.2 0.8 copy.63
  45.0 20.7 %all-to-all-done.1 = bf16[1,8,64,288]{3,2,0,1:T(8,128)(2,1)S(1)} async-done(((bf16[1,8,64,288]{3,2,0,1:T(8,128)(2,1)}), bf16[1,8,64,288]{3,2,0,1:T(8,128)(2,1)S(1)}, u32[]{:S(2)}, u32[]{:S(2)}) %all-to-all-start.1) | async-done | bytes 294944 | tf_op jit(solution)/shard_map/all_to_all | solution.py:93
  65.7 3.5 %all-to-all-start.3 = ((bf16[1,8,64,288]{3,2,0,1:T(8,128)(2,1)}), bf16[1,8,64,288]{3,2,0,1:T(8,128)(2,1)S(1)}, u32[]{:S(2)}, u32[]{:S(2)}) async-start(bf16[1,8,64,288]{3,2,0,1:T(8,128)(2,1)} %bitcast.12), calls=%async_computation.3 | async-start | bytes 786432 | tf_op jit(solution)/shard_map/all_to_all | solution.py:93
  69.2 20.1 %all-gather.2.cloned.1.call-done = bf16[1152,1152]{1,0:T(8,128)(2,1)} async-done(((bf16[288,1152]{1,0:T(8,128)(2,1)}), bf16[1152,1152]{1,0:T(8,128)(2,1)}) %all-gather.2.cloned.1.call-update) | async-done | bytes 2654224 | tf_op jit(solution)/shard_map/all_gather | solution.py:84
  89.3 0.0 copy-done.1
  89.3 0.0 copy-done.5
  89.3 2.7 %convolution_convert_fusion = bf16[128,1152]{1,0:T(8,128)(2,1)S(1)} fusion(bf16[1152,1152]{1,0:T(8,128)(2,1)} %all-gather.2.cloned.1.call-done, bf16[1,128,1152]{2,1,0:T(8,128)(2,1)S(1)} %copy-done.1, f32[1152]{0:T(1024)S(1)} %copy-done.5), kind=kOutput, calls=%fused_computation.2 | convolution fusion | flops 340328448 | bytes 3248640 | tf_op jit(solution)/shard_map/dot_general | solution.py:82
  91.9 0.4 reshape.84
  92.3 0.8 copy.61
  93.1 0.0 all-to-all-done.3
  93.1 3.5 %all-to-all-start.2 = ((bf16[1,8,64,288]{3,2,0,1:T(8,128)(2,1)}), bf16[1,8,64,288]{3,2,0,1:T(8,128)(2,1)S(1)}, u32[]{:S(2)}, u32[]{:S(2)}) async-start(bf16[1,8,64,288]{3,2,0,1:T(8,128)(2,1)} %bitcast.9), calls=%async_computation.2 | async-start | bytes 786432 | tf_op jit(solution)/shard_map/all_to_all | solution.py:93
  96.6 0.3 reshape_reshape.24
  97.0 0.3 reshape_reshape.25
  97.3 1.1 reshape_reshape.27
  98.4 2.1 %fusion.36 = (f32[64,4,8]{2,1,0:T(4,128)S(1)}, f32[64,4,8,8]{2,3,1,0:T(8,128)}) fusion(bf16[8,64,4,72]{3,2,1,0:T(4,128)(2,1)S(1)} %reshape_reshape.25, bf16[8,64,4,72]{3,2,1,0:T(4,128)(2,1)S(1)} %reshape_reshape.24), kind=kOutput, calls=%fused_computation.37 | convolution fusion | flops 2408455 | bytes 663552 | tf_op jit(solution)/shard_map/sub | solution.py:30
  100.5 8.1 %all-to-all-done.2 = bf16[1,8,64,288]{3,2,0,1:T(8,128)(2,1)S(1)} async-done(((bf16[1,8,64,288]{3,2,0,1:T(8,128)(2,1)}), bf16[1,8,64,288]{3,2,0,1:T(8,128)(2,1)S(1)}, u32[]{:S(2)}, u32[]{:S(2)}) %all-to-all-start.2) | async-done | bytes 294944 | tf_op jit(solution)/shard_map/all_to_all | solution.py:93
  108.6 0.3 reshape_reshape.26
  108.9 0.0 copy-start.2
  108.9 0.0 copy-start.6
  109.0 3.1 %multiply_reduce_fusion = (f32[8,64,4]{0,2,1:T(4,128)S(1)}, bf16[8,64,4,72]{3,0,2,1:T(8,128)(2,1)}) fusion(bf16[8,64,4,72]{3,2,1,0:T(4,128)(2,1)S(1)} %reshape_reshape.26, bf16[8,64,4,72]{3,2,1,0:T(4,128)(2,1)} %reshape_reshape.27, f32[64,4,8,8]{2,3,1,0:T(8,128)} %get-tuple-element.5, f32[64,4,8]{2,1,0:T(4,128)S(1)} %get-tuple-element.4), kind=kOutput, calls=%fused_computation.19 | convolution fusion | flops 3127296 | bytes 966656 | tf_op jit(solution)/shard_map/phfg,gphd->fphd/dot_general | solution.py:33
  112.1 0.8 fusion.5
  112.9 0.5 fusion.8
  113.4 0.2 copy.77
  113.6 1.1 reshape_reshape.29
  114.7 3.6 %all-to-all-start.5 = ((bf16[8,1,64,288]{3,2,1,0:T(8,128)(2,1)}), bf16[8,1,64,288]{3,2,1,0:T(8,128)(2,1)S(1)}, u32[]{:S(2)}, u32[]{:S(2)}) async-start(bf16[8,1,64,288]{3,2,1,0:T(8,128)(2,1)} %bitcast.20), calls=%async_computation.5 | async-start | bytes 786432 | tf_op jit(solution)/shard_map/all_to_all | solution.py:101
  118.3 0.5 fusion.7
  118.9 0.2 copy.73
  119.1 1.1 reshape_reshape.28
  120.2 10.0 %all-to-all-done.5 = bf16[8,1,64,288]{3,2,1,0:T(8,128)(2,1)S(1)} async-done(((bf16[8,1,64,288]{3,2,1,0:T(8,128)(2,1)}), bf16[8,1,64,288]{3,2,1,0:T(8,128)(2,1)S(1)}, u32[]{:S(2)}, u32[]{:S(2)}) %all-to-all-start.5) | async-done | bytes 294944 | tf_op jit(solution)/shard_map/all_to_all | solution.py:101
  130.2 3.6 %all-to-all-start.4 = ((bf16[8,1,64,288]{3,2,1,0:T(8,128)(2,1)}), bf16[8,1,64,288]{3,2,1,0:T(8,128)(2,1)S(1)}, u32[]{:S(2)}, u32[]{:S(2)}) async-start(bf16[8,1,64,288]{3,2,1,0:T(8,128)(2,1)} %bitcast.16), calls=%async_computation.4 | async-start | bytes 786432 | tf_op jit(solution)/shard_map/all_to_all | solution.py:101
  133.8 1.2 copy.84
  135.1 1.1 reshape_reshape.31
  136.2 9.4 %all-to-all-done.4 = bf16[8,1,64,288]{3,2,1,0:T(8,128)(2,1)S(1)} async-done(((bf16[8,1,64,288]{3,2,1,0:T(8,128)(2,1)}), bf16[8,1,64,288]{3,2,1,0:T(8,128)(2,1)S(1)}, u32[]{:S(2)}, u32[]{:S(2)}) %all-to-all-start.4) | async-done | bytes 294944 | tf_op jit(solution)/shard_map/all_to_all | solution.py:101
  145.6 4.1 %all-to-all-start.7 = ((bf16[8,1,64,288]{3,2,1,0:T(8,128)(2,1)}), bf16[8,1,64,288]{3,2,1,0:T(8,128)(2,1)}, u32[]{:S(2)}, u32[]{:S(2)}) async-start(bf16[8,1,64,288]{3,2,1,0:T(8,128)(2,1)} %bitcast.28), calls=%async_computation.7 | async-start | bytes 786432 | tf_op jit(solution)/shard_map/all_to_all | solution.py:101
  149.7 1.8 fusion.9
  151.5 0.2 copy.81
  151.7 1.1 reshape_reshape.30
  152.8 8.3 %all-to-all-done.7 = bf16[8,1,64,288]{3,2,1,0:T(8,128)(2,1)} async-done(((bf16[8,1,64,288]{3,2,1,0:T(8,128)(2,1)}), bf16[8,1,64,288]{3,2,1,0:T(8,128)(2,1)}, u32[]{:S(2)}, u32[]{:S(2)}) %all-to-all-start.7) | async-done | bytes 294944 | tf_op jit(solution)/shard_map/all_to_all | solution.py:101
  161.1 4.3 %all-to-all-start.6 = ((bf16[8,1,64,288]{3,2,1,0:T(8,128)(2,1)}), bf16[8,1,64,288]{3,2,1,0:T(8,128)(2,1)}, u32[]{:S(2)}, u32[]{:S(2)}) async-start(bf16[8,1,64,288]{3,2,1,0:T(8,128)(2,1)} %bitcast.73), calls=%async_computation.6 | async-start | bytes 786432 | tf_op jit(solution)/shard_map/all_to_all | solution.py:101
  165.4 1.1 copy.79
  166.4 2.0 %reshape.90 = bf16[1,128,1152]{2,1,0:T(8,128)(2,1)} reshape(bf16[2,64,4,288]{3,2,1,0:T(4,128)(2,1)} %copy.79) | data formatting | bytes 589824 | tf_op jit(solution)/shard_map/reshape | solution.py:69
  168.5 0.3 copy.75
  168.8 1.0 reshape.88
  169.8 1.3 copy.122
  171.1 0.3 squeeze_reshape.3
  171.4 1.6 fusion.10
  172.9 22.4 %psum.7 = f32[1152]{0:T(1024)} all-reduce(f32[1152]{0:T(1024)S(1)} %fusion.10), channel_id=1, replica_groups=mesh['clip'=4,'tx'=4,'ty'=2] {'tx','ty'}, use_global_device_ids=true, to_apply=%region_4.0 | all-reduce | flops 1152 | bytes 9216 | tf_op jit(solution)/shard_map/psum | solution.py:113
  195.4 0.0 all-to-all-done.6
  195.4 1.3 copy.83
  196.7 1.0 reshape.92
  (6 shorter events, 0.0 us)
Async XLA Ops:
  7.2 10.3 %copy-start.3 = (bf16[1,128,1152]{2,1,0:T(8,128)(2,1)S(1)}, bf16[1,128,1152]{2,1,0:T(8,128)(2,1)}, u32[]{:S(2)}) copy-start(bf16[1,128,1152]{2,1,0:T(8,128)(2,1)} %param.7) | copy-start | bytes 884740
  7.2 36.7 %copy-start.4 = (bf16[1,128,1152]{2,1,0:T(8,128)(2,1)S(1)}, bf16[1,128,1152]{2,1,0:T(8,128)(2,1)}, u32[]{:S(2)}) copy-start(bf16[1,128,1152]{2,1,0:T(8,128)(2,1)} %param.8) | copy-start | bytes 884740
  7.2 82.1 %all-gather.2.cloned.1.call-start = ((), (), s32[]{:S(2)}) async-start(), calls=%async_computation.8 | async-start | bytes 3317760 | tf_op jit(solution)/shard_map/all_gather | solution.py:84
  10.1 79.2 %copy-start.1 = (bf16[1,128,1152]{2,1,0:T(8,128)(2,1)S(1)}, bf16[1,128,1152]{2,1,0:T(8,128)(2,1)}, u32[]{:S(2)}) copy-start(bf16[1,128,1152]{2,1,0:T(8,128)(2,1)} %param.9) | copy-start | bytes 884740
  10.1 79.2 %copy-start.5 = (f32[1152]{0:T(1024)S(1)}, f32[1152]{0:T(1024)}, u32[]{:S(2)}) copy-start(f32[1152]{0:T(1024)} %param.10) | copy-start | bytes 13828
  10.1 27.7 %all-to-all-start = ((bf16[1,8,64,288]{3,2,0,1:T(8,128)(2,1)}), bf16[1,8,64,288]{3,2,0,1:T(8,128)(2,1)S(1)}, u32[]{:S(2)}, u32[]{:S(2)}) async-start(bf16[1,8,64,288]{3,2,0,1:T(8,128)(2,1)} %bitcast.2), calls=%async_computation | async-start | bytes 786432 | tf_op jit(solution)/shard_map/all_to_all | solution.py:93
  37.8 28.0 %all-to-all-start.1 = ((bf16[1,8,64,288]{3,2,0,1:T(8,128)(2,1)}), bf16[1,8,64,288]{3,2,0,1:T(8,128)(2,1)S(1)}, u32[]{:S(2)}, u32[]{:S(2)}) async-start(bf16[1,8,64,288]{3,2,0,1:T(8,128)(2,1)} %bitcast.5), calls=%async_computation.1 | async-start | bytes 786432 | tf_op jit(solution)/shard_map/all_to_all | solution.py:93
  65.7 27.4 %all-to-all-start.3 = ((bf16[1,8,64,288]{3,2,0,1:T(8,128)(2,1)}), bf16[1,8,64,288]{3,2,0,1:T(8,128)(2,1)S(1)}, u32[]{:S(2)}, u32[]{:S(2)}) async-start(bf16[1,8,64,288]{3,2,0,1:T(8,128)(2,1)} %bitcast.12), calls=%async_computation.3 | async-start | bytes 786432 | tf_op jit(solution)/shard_map/all_to_all | solution.py:93
  93.1 15.5 %all-to-all-start.2 = ((bf16[1,8,64,288]{3,2,0,1:T(8,128)(2,1)}), bf16[1,8,64,288]{3,2,0,1:T(8,128)(2,1)S(1)}, u32[]{:S(2)}, u32[]{:S(2)}) async-start(bf16[1,8,64,288]{3,2,0,1:T(8,128)(2,1)} %bitcast.9), calls=%async_computation.2 | async-start | bytes 786432 | tf_op jit(solution)/shard_map/all_to_all | solution.py:93
  108.9 3.1 %copy-start.2 = (bf16[8,64,4,72]{3,2,1,0:T(4,128)(2,1)S(1)}, bf16[8,64,4,72]{3,2,1,0:T(4,128)(2,1)}, u32[]{:S(2)}) copy-start(bf16[8,64,4,72]{3,2,1,0:T(4,128)(2,1)} %reshape_reshape.27) | copy-start | bytes 884740
  108.9 3.1 %copy-start.6 = (f32[64,4,8,8]{2,3,1,0:T(8,128)S(1)}, f32[64,4,8,8]{2,3,1,0:T(8,128)}, u32[]{:S(2)}) copy-start(f32[64,4,8,8]{2,3,1,0:T(8,128)} %get-tuple-element.5) | copy-start | bytes 196612
  114.7 15.5 %all-to-all-start.5 = ((bf16[8,1,64,288]{3,2,1,0:T(8,128)(2,1)}), bf16[8,1,64,288]{3,2,1,0:T(8,128)(2,1)S(1)}, u32[]{:S(2)}, u32[]{:S(2)}) async-start(bf16[8,1,64,288]{3,2,1,0:T(8,128)(2,1)} %bitcast.20), calls=%async_computation.5 | async-start | bytes 786432 | tf_op jit(solution)/shard_map/all_to_all | solution.py:101
  130.2 15.4 %all-to-all-start.4 = ((bf16[8,1,64,288]{3,2,1,0:T(8,128)(2,1)}), bf16[8,1,64,288]{3,2,1,0:T(8,128)(2,1)S(1)}, u32[]{:S(2)}, u32[]{:S(2)}) async-start(bf16[8,1,64,288]{3,2,1,0:T(8,128)(2,1)} %bitcast.16), calls=%async_computation.4 | async-start | bytes 786432 | tf_op jit(solution)/shard_map/all_to_all | solution.py:101
  145.6 15.5 %all-to-all-start.7 = ((bf16[8,1,64,288]{3,2,1,0:T(8,128)(2,1)}), bf16[8,1,64,288]{3,2,1,0:T(8,128)(2,1)}, u32[]{:S(2)}, u32[]{:S(2)}) async-start(bf16[8,1,64,288]{3,2,1,0:T(8,128)(2,1)} %bitcast.28), calls=%async_computation.7 | async-start | bytes 786432 | tf_op jit(solution)/shard_map/all_to_all | solution.py:101
  152.8 18.6 %copy-start = (bf16[1152,1152]{1,0:T(8,128)(2,1)S(1)}, bf16[1152,1152]{1,0:T(8,128)(2,1)}, u32[]{:S(2)}) copy-start(bf16[1152,1152]{1,0:T(8,128)(2,1)} %all-gather.2.cloned.1.call-done) | copy-start | bytes 7962628
  161.1 34.3 %all-to-all-start.6 = ((bf16[8,1,64,288]{3,2,1,0:T(8,128)(2,1)}), bf16[8,1,64,288]{3,2,1,0:T(8,128)(2,1)}, u32[]{:S(2)}, u32[]{:S(2)}) async-start(bf16[8,1,64,288]{3,2,1,0:T(8,128)(2,1)} %bitcast.73), calls=%async_computation.6 | async-start | bytes 786432 | tf_op jit(solution)/shard_map/all_to_all | solution.py:101
Sparse Core Ops, SparseCore 0:
  9.6 79.6 all-gather.1
where the time goes:
time: 206 us; the launch traced here: 205 us
  waiting for transfers between devices  96.3 us (47%)
  starting transfers between devices  36.2 us (18%)
  blocking collectives  22.4 us (11%)
  local copies, waits for them, and re-layouts  22.3 us (11%)
  between operations  14.2 us (7%)
  matrix products  13 us (6%)
    all_to_all x4, waiting for transfers between devices, per_device(): lax.all_to_all(shortened(prepared), ('tx', 'ty'), split_axis=1, concat_ax...  47.9 us
    all_to_all x4, waiting for transfers between devices, per_device(): lax.all_to_all(shortened(outgoing), ('tx', 'ty'), split_axis=0, concat_ax...  27.7 us
    psum x1, blocking collectives, per_device(): gate_grad = lax.psum(local_terms, ('tx', 'ty'))  22.4 us
    all_to_all x4, starting transfers between devices, per_device(): lax.all_to_all(shortened(prepared), ('tx', 'ty'), split_axis=1, concat_ax...  20.5 us
    all_gather x1, waiting for transfers between devices, per_device(): lax.all_gather(out_weight, 'tx', axis=0, tiled=True)  20.1 us
    all_to_all x4, starting transfers between devices, per_device(): lax.all_to_all(shortened(outgoing), ('tx', 'ty'), split_axis=0, concat_ax...  15.6 us
    another operation x4, local copies, waits for them, and re-layouts, per_device(): arr.reshape(devices_here, 1, block_pos, block_width)  4.46 us
  transfers between devices with their start and end apart: 9, of which 7 were waited for; matrix products, arithmetic and copies ran while one was open for 13% of the time, Pallas kernels for 0%

commit v1 on v0

--- a/solution.py
+++ b/solution.py
@@ -2,6 +2,7 @@
 import jax.numpy as jnp
 from jax import lax
 from jax.sharding import PartitionSpec as P
+from jax.lax import all_gather
 
 HEAD_DIM = 72
 
@@ -110,7 +111,7 @@
         preferred_element_type=jnp.float32,
     )
     local_terms = jnp.sum(grad_rows.astype(jnp.float32) * branch_out, axis=0)
-    gate_grad = lax.psum(local_terms, ("tx", "ty"))
+    gate_grad = jnp.sum(all_gather(local_terms, ("tx", "ty")), 0)
     return (query_grad, key_grad, value_grad, gate_grad)
 
 

time: 206 us -> 215 us (1.044)
  blocking collectives: 22.4 us -> 31 us
    all_gather x0 -> x1, blocking collectives: none -> 31 us  [per_device(): gate_grad = jnp.sum(all_gather(local_terms, ('tx', 'ty')), 0)]
    psum x1 -> x0, blocking collectives: 22.4 us -> none  [per_device(): gate_grad = lax.psum(local_terms, ('tx', 'ty'))]
  transfers between devices with their start and end apart: 9 -> 9, of which waited for: 7 -> 7; matrix products, arithmetic and copies ran while one was open for 13% -> 12% of each run, Pallas kernels for 0% -> 0%
where the time goes in v1:
time: 215 us; the launch traced here: 214 us
  waiting for transfers between devices  97 us (45%)
  starting transfers between devices  36.2 us (17%)
  blocking collectives  31 us (14%)
  local copies, waits for them, and re-layouts  21.6 us (10%)
  between operations  14.2 us (7%)
  matrix products  12.9 us (6%)
    all_to_all x4, waiting for transfers between devices, per_device(): lax.all_to_all(shortened(prepared), ('tx', 'ty'), split_axis=1, concat_ax...  48.7 us
    all_gather x1, blocking collectives, per_device(): gate_grad = jnp.sum(all_gather(local_terms, ('tx', 'ty')), 0)  31 us
    all_to_all x4, waiting for transfers between devices, per_device(): lax.all_to_all(shortened(outgoing), ('tx', 'ty'), split_axis=0, concat_ax...  27.6 us
    all_to_all x4, starting transfers between devices, per_device(): lax.all_to_all(shortened(prepared), ('tx', 'ty'), split_axis=1, concat_ax...  20.5 us
    all_gather x1, waiting for transfers between devices, per_device(): lax.all_gather(out_weight, 'tx', axis=0, tiled=True)  20.1 us
    all_to_all x4, starting transfers between devices, per_device(): lax.all_to_all(shortened(outgoing), ('tx', 'ty'), split_axis=0, concat_ax...  15.6 us
    another operation x4, local copies, waits for them, and re-layouts, per_device(): arr.reshape(devices_here, 1, block_pos, block_width)  4.49 us
  transfers between devices with their start and end apart: 9, of which 7 were waited for; matrix products, arithmetic and copies ran while one was open for 12% of the time, Pallas kernels for 0%

profile of v1, /device:TPU:0, one launch (start us, length us, event | category | flops | bytes accessed | tf_op | source)
XLA Modules:
  0.0 213.6 jit_solution(14213414870181917854)
XLA Ops:
  7.2 0.0 copy-start.2
  7.2 0.0 copy-start.3
  7.2 0.0 all-gather.4.cloned.1.call-start
  7.2 0.7 all-gather.4.cloned.1.call-update
  7.9 1.3 reshape_squeeze.9
  9.2 0.8 copy.55
  10.1 7.4 %all-to-all-start = ((bf16[1,8,64,288]{3,2,0,1:T(8,128)(2,1)}), bf16[1,8,64,288]{3,2,0,1:T(8,128)(2,1)S(1)}, u32[]{:S(2)}, u32[]{:S(2)}) async-start(bf16[1,8,64,288]{3,2,0,1:T(8,128)(2,1)} %bitcast.2), calls=%async_computation | async-start | bytes 786432 | tf_op jit(solution)/shard_map/all_to_all | solution.py:94
  17.5 0.0 copy-done.2
  17.5 0.4 reshape_squeeze.10
  17.9 0.8 copy.57
  18.7 19.1 %all-to-all-done = bf16[1,8,64,288]{3,2,0,1:T(8,128)(2,1)S(1)} async-done(((bf16[1,8,64,288]{3,2,0,1:T(8,128)(2,1)}), bf16[1,8,64,288]{3,2,0,1:T(8,128)(2,1)S(1)}, u32[]{:S(2)}, u32[]{:S(2)}) %all-to-all-start) | async-done | bytes 294944 | tf_op jit(solution)/shard_map/all_to_all | solution.py:94
  37.8 6.1 %all-to-all-start.1 = ((bf16[1,8,64,288]{3,2,0,1:T(8,128)(2,1)}), bf16[1,8,64,288]{3,2,0,1:T(8,128)(2,1)S(1)}, u32[]{:S(2)}, u32[]{:S(2)}) async-start(bf16[1,8,64,288]{3,2,0,1:T(8,128)(2,1)} %bitcast.5), calls=%async_computation.1 | async-start | bytes 786432 | tf_op jit(solution)/shard_map/all_to_all | solution.py:94
  43.9 0.0 copy-done.3
  43.9 0.4 reshape_squeeze.11
  44.2 0.8 copy.63
  45.1 20.7 %all-to-all-done.1 = bf16[1,8,64,288]{3,2,0,1:T(8,128)(2,1)S(1)} async-done(((bf16[1,8,64,288]{3,2,0,1:T(8,128)(2,1)}), bf16[1,8,64,288]{3,2,0,1:T(8,128)(2,1)S(1)}, u32[]{:S(2)}, u32[]{:S(2)}) %all-to-all-start.1) | async-done | bytes 294944 | tf_op jit(solution)/shard_map/all_to_all | solution.py:94
  65.8 3.5 %all-to-all-start.3 = ((bf16[1,8,64,288]{3,2,0,1:T(8,128)(2,1)}), bf16[1,8,64,288]{3,2,0,1:T(8,128)(2,1)S(1)}, u32[]{:S(2)}, u32[]{:S(2)}) async-start(bf16[1,8,64,288]{3,2,0,1:T(8,128)(2,1)} %bitcast.12), calls=%async_computation.3 | async-start | bytes 786432 | tf_op jit(solution)/shard_map/all_to_all | solution.py:94
  69.2 20.1 %all-gather.4.cloned.1.call-done = bf16[1152,1152]{1,0:T(8,128)(2,1)} async-done(((bf16[288,1152]{1,0:T(8,128)(2,1)}), bf16[1152,1152]{1,0:T(8,128)(2,1)}) %all-gather.4.cloned.1.call-update) | async-done | bytes 2654224 | tf_op jit(solution)/shard_map/all_gather | solution.py:85
  89.3 0.0 copy-done.1
  89.3 0.0 copy-done.4
  89.3 2.7 %convolution_convert_fusion = bf16[128,1152]{1,0:T(8,128)(2,1)S(1)} fusion(bf16[1152,1152]{1,0:T(8,128)(2,1)} %all-gather.4.cloned.1.call-done, bf16[1,128,1152]{2,1,0:T(8,128)(2,1)S(1)} %copy-done.1, f32[1152]{0:T(1024)S(1)} %copy-done.4), kind=kOutput, calls=%fused_computation.2 | convolution fusion | flops 340328448 | bytes 3248640 | tf_op jit(solution)/shard_map/dot_general | solution.py:83
  92.0 0.4 reshape.84
  92.3 0.8 copy.61
  93.1 0.0 all-to-all-done.3
  93.1 3.5 %all-to-all-start.2 = ((bf16[1,8,64,288]{3,2,0,1:T(8,128)(2,1)}), bf16[1,8,64,288]{3,2,0,1:T(8,128)(2,1)S(1)}, u32[]{:S(2)}, u32[]{:S(2)}) async-start(bf16[1,8,64,288]{3,2,0,1:T(8,128)(2,1)} %bitcast.9), calls=%async_computation.2 | async-start | bytes 786432 | tf_op jit(solution)/shard_map/all_to_all | solution.py:94
  96.7 0.3 reshape_reshape.24
  97.0 0.3 reshape_reshape.25
  97.3 0.3 reshape_reshape.27
  97.7 2.1 fusion.36
  99.8 8.8 %all-to-all-done.2 = bf16[1,8,64,288]{3,2,0,1:T(8,128)(2,1)S(1)} async-done(((bf16[1,8,64,288]{3,2,0,1:T(8,128)(2,1)}), bf16[1,8,64,288]{3,2,0,1:T(8,128)(2,1)S(1)}, u32[]{:S(2)}, u32[]{:S(2)}) %all-to-all-start.2) | async-done | bytes 294944 | tf_op jit(solution)/shard_map/all_to_all | solution.py:94
  108.6 0.3 reshape_reshape.26
  109.0 2.9 %multiply_reduce_fusion = (f32[8,64,4]{0,2,1:T(4,128)S(1)}, bf16[8,64,4,72]{3,0,2,1:T(8,128)(2,1)}) fusion(bf16[8,64,4,72]{3,2,1,0:T(4,128)(2,1)S(1)} %reshape_reshape.26, bf16[8,64,4,72]{3,2,1,0:T(4,128)(2,1)S(1)} %reshape_reshape.27, f32[64,4,8,8]{2,3,1,0:T(8,128)} %get-tuple-element.5, f32[64,4,8]{2,1,0:T(4,128)S(1)} %get-tuple-element.4), kind=kOutput, calls=%fused_computation.19 | convolution fusion | flops 3127296 | bytes 966656 | tf_op jit(solution)/shard_map/phfg,gphd->fphd/dot_general | solution.py:34
  111.9 0.0 copy-done.5
  111.9 0.9 fusion.5
  112.8 0.5 fusion.8
  113.2 0.2 copy.77
  113.5 1.1 reshape_reshape.29
  114.6 3.6 %all-to-all-start.5 = ((bf16[8,1,64,288]{3,2,1,0:T(8,128)(2,1)}), bf16[8,1,64,288]{3,2,1,0:T(8,128)(2,1)S(1)}, u32[]{:S(2)}, u32[]{:S(2)}) async-start(bf16[8,1,64,288]{3,2,1,0:T(8,128)(2,1)} %bitcast.20), calls=%async_computation.5 | async-start | bytes 786432 | tf_op jit(solution)/shard_map/all_to_all | solution.py:102
  118.2 0.5 fusion.7
  118.7 0.2 copy.73
  118.9 1.1 reshape_reshape.28
  120.1 10.0 %all-to-all-done.5 = bf16[8,1,64,288]{3,2,1,0:T(8,128)(2,1)S(1)} async-done(((bf16[8,1,64,288]{3,2,1,0:T(8,128)(2,1)}), bf16[8,1,64,288]{3,2,1,0:T(8,128)(2,1)S(1)}, u32[]{:S(2)}, u32[]{:S(2)}) %all-to-all-start.5) | async-done | bytes 294944 | tf_op jit(solution)/shard_map/all_to_all | solution.py:102
  130.0 3.6 %all-to-all-start.4 = ((bf16[8,1,64,288]{3,2,1,0:T(8,128)(2,1)}), bf16[8,1,64,288]{3,2,1,0:T(8,128)(2,1)S(1)}, u32[]{:S(2)}, u32[]{:S(2)}) async-start(bf16[8,1,64,288]{3,2,1,0:T(8,128)(2,1)} %bitcast.16), calls=%async_computation.4 | async-start | bytes 786432 | tf_op jit(solution)/shard_map/all_to_all | solution.py:102
  133.7 1.2 copy.84
  134.9 1.1 reshape_reshape.31
  136.0 9.4 %all-to-all-done.4 = bf16[8,1,64,288]{3,2,1,0:T(8,128)(2,1)S(1)} async-done(((bf16[8,1,64,288]{3,2,1,0:T(8,128)(2,1)}), bf16[8,1,64,288]{3,2,1,0:T(8,128)(2,1)S(1)}, u32[]{:S(2)}, u32[]{:S(2)}) %all-to-all-start.4) | async-done | bytes 294944 | tf_op jit(solution)/shard_map/all_to_all | solution.py:102
  145.5 4.1 %all-to-all-start.7 = ((bf16[8,1,64,288]{3,2,1,0:T(8,128)(2,1)}), bf16[8,1,64,288]{3,2,1,0:T(8,128)(2,1)}, u32[]{:S(2)}, u32[]{:S(2)}) async-start(bf16[8,1,64,288]{3,2,1,0:T(8,128)(2,1)} %bitcast.28), calls=%async_computation.7 | async-start | bytes 786432 | tf_op jit(solution)/shard_map/all_to_all | solution.py:102
  149.6 1.8 fusion.9
  151.3 0.2 copy.81
  151.5 1.1 reshape_reshape.30
  152.7 8.2 %all-to-all-done.7 = bf16[8,1,64,288]{3,2,1,0:T(8,128)(2,1)} async-done(((bf16[8,1,64,288]{3,2,1,0:T(8,128)(2,1)}), bf16[8,1,64,288]{3,2,1,0:T(8,128)(2,1)}, u32[]{:S(2)}, u32[]{:S(2)}) %all-to-all-start.7) | async-done | bytes 294944 | tf_op jit(solution)/shard_map/all_to_all | solution.py:102
  160.9 4.3 %all-to-all-start.6 = ((bf16[8,1,64,288]{3,2,1,0:T(8,128)(2,1)}), bf16[8,1,64,288]{3,2,1,0:T(8,128)(2,1)}, u32[]{:S(2)}, u32[]{:S(2)}) async-start(bf16[8,1,64,288]{3,2,1,0:T(8,128)(2,1)} %bitcast.73), calls=%async_computation.6 | async-start | bytes 786432 | tf_op jit(solution)/shard_map/all_to_all | solution.py:102
  165.2 1.1 copy.79
  166.3 2.0 reshape.90
  168.3 0.3 copy.75
  168.6 1.0 reshape.88
  169.6 1.3 copy.122
  170.9 0.3 squeeze_reshape.3
  171.2 1.6 fusion.10
  172.8 31.0 %all-gather.1 = f32[8,1,1152]{2,1,0:T(1,128)S(1)} all-gather(f32[1,1,1152]{2,1,0:T(1,128)S(1)} %reshape.96), channel_id=2, replica_groups=mesh['clip'=4,'tx'=4,'ty'=2] {'tx','ty'}, dimensions={0}, use_global_device_ids=true | all-gather | bytes 41472 | tf_op jit(solution)/shard_map/all_gather | solution.py:114
  203.8 0.0 all-to-all-done.6
  203.8 1.3 copy.83
  205.1 1.0 reshape.92
  206.1 0.6 reduce_sum.39
  (6 shorter events, 0.0 us)
Async XLA Ops:
  7.2 10.4 %copy-start.2 = (bf16[1,128,1152]{2,1,0:T(8,128)(2,1)S(1)}, bf16[1,128,1152]{2,1,0:T(8,128)(2,1)}, u32[]{:S(2)}) copy-start(bf16[1,128,1152]{2,1,0:T(8,128)(2,1)} %param.7) | copy-start | bytes 884740
  7.2 36.7 %copy-start.3 = (bf16[1,128,1152]{2,1,0:T(8,128)(2,1)S(1)}, bf16[1,128,1152]{2,1,0:T(8,128)(2,1)}, u32[]{:S(2)}) copy-start(bf16[1,128,1152]{2,1,0:T(8,128)(2,1)} %param.8) | copy-start | bytes 884740
  7.2 82.1 %all-gather.4.cloned.1.call-start = ((), (), s32[]{:S(2)}) async-start(), calls=%async_computation.8 | async-start | bytes 3317760 | tf_op jit(solution)/shard_map/all_gather | solution.py:85
  10.1 79.2 %copy-start.1 = (bf16[1,128,1152]{2,1,0:T(8,128)(2,1)S(1)}, bf16[1,128,1152]{2,1,0:T(8,128)(2,1)}, u32[]{:S(2)}) copy-start(bf16[1,128,1152]{2,1,0:T(8,128)(2,1)} %param.9) | copy-start | bytes 884740
  10.1 79.2 %copy-start.4 = (f32[1152]{0:T(1024)S(1)}, f32[1152]{0:T(1024)}, u32[]{:S(2)}) copy-start(f32[1152]{0:T(1024)} %param.10) | copy-start | bytes 13828
  10.1 27.7 %all-to-all-start = ((bf16[1,8,64,288]{3,2,0,1:T(8,128)(2,1)}), bf16[1,8,64,288]{3,2,0,1:T(8,128)(2,1)S(1)}, u32[]{:S(2)}, u32[]{:S(2)}) async-start(bf16[1,8,64,288]{3,2,0,1:T(8,128)(2,1)} %bitcast.2), calls=%async_computation | async-start | bytes 786432 | tf_op jit(solution)/shard_map/all_to_all | solution.py:94
  37.8 28.0 %all-to-all-start.1 = ((bf16[1,8,64,288]{3,2,0,1:T(8,128)(2,1)}), bf16[1,8,64,288]{3,2,0,1:T(8,128)(2,1)S(1)}, u32[]{:S(2)}, u32[]{:S(2)}) async-start(bf16[1,8,64,288]{3,2,0,1:T(8,128)(2,1)} %bitcast.5), calls=%async_computation.1 | async-start | bytes 786432 | tf_op jit(solution)/shard_map/all_to_all | solution.py:94
  65.8 27.4 %all-to-all-start.3 = ((bf16[1,8,64,288]{3,2,0,1:T(8,128)(2,1)}), bf16[1,8,64,288]{3,2,0,1:T(8,128)(2,1)S(1)}, u32[]{:S(2)}, u32[]{:S(2)}) async-start(bf16[1,8,64,288]{3,2,0,1:T(8,128)(2,1)} %bitcast.12), calls=%async_computation.3 | async-start | bytes 786432 | tf_op jit(solution)/shard_map/all_to_all | solution.py:94
  93.1 15.5 %all-to-all-start.2 = ((bf16[1,8,64,288]{3,2,0,1:T(8,128)(2,1)}), bf16[1,8,64,288]{3,2,0,1:T(8,128)(2,1)S(1)}, u32[]{:S(2)}, u32[]{:S(2)}) async-start(bf16[1,8,64,288]{3,2,0,1:T(8,128)(2,1)} %bitcast.9), calls=%async_computation.2 | async-start | bytes 786432 | tf_op jit(solution)/shard_map/all_to_all | solution.py:94
  109.0 3.0 %copy-start.5 = (f32[64,4,8,8]{2,3,1,0:T(8,128)S(1)}, f32[64,4,8,8]{2,3,1,0:T(8,128)}, u32[]{:S(2)}) copy-start(f32[64,4,8,8]{2,3,1,0:T(8,128)} %get-tuple-element.5) | copy-start | bytes 196612
  114.6 15.5 %all-to-all-start.5 = ((bf16[8,1,64,288]{3,2,1,0:T(8,128)(2,1)}), bf16[8,1,64,288]{3,2,1,0:T(8,128)(2,1)S(1)}, u32[]{:S(2)}, u32[]{:S(2)}) async-start(bf16[8,1,64,288]{3,2,1,0:T(8,128)(2,1)} %bitcast.20), calls=%async_computation.5 | async-start | bytes 786432 | tf_op jit(solution)/shard_map/all_to_all | solution.py:102
  130.0 15.4 %all-to-all-start.4 = ((bf16[8,1,64,288]{3,2,1,0:T(8,128)(2,1)}), bf16[8,1,64,288]{3,2,1,0:T(8,128)(2,1)S(1)}, u32[]{:S(2)}, u32[]{:S(2)}) async-start(bf16[8,1,64,288]{3,2,1,0:T(8,128)(2,1)} %bitcast.16), calls=%async_computation.4 | async-start | bytes 786432 | tf_op jit(solution)/shard_map/all_to_all | solution.py:102
  145.5 15.5 %all-to-all-start.7 = ((bf16[8,1,64,288]{3,2,1,0:T(8,128)(2,1)}), bf16[8,1,64,288]{3,2,1,0:T(8,128)(2,1)}, u32[]{:S(2)}, u32[]{:S(2)}) async-start(bf16[8,1,64,288]{3,2,1,0:T(8,128)(2,1)} %bitcast.28), calls=%async_computation.7 | async-start | bytes 786432 | tf_op jit(solution)/shard_map/all_to_all | solution.py:102
  152.7 18.5 %copy-start = (bf16[1152,1152]{1,0:T(8,128)(2,1)S(1)}, bf16[1152,1152]{1,0:T(8,128)(2,1)}, u32[]{:S(2)}) copy-start(bf16[1152,1152]{1,0:T(8,128)(2,1)} %all-gather.4.cloned.1.call-done) | copy-start | bytes 7962628
  160.9 42.9 %all-to-all-start.6 = ((bf16[8,1,64,288]{3,2,1,0:T(8,128)(2,1)}), bf16[8,1,64,288]{3,2,1,0:T(8,128)(2,1)}, u32[]{:S(2)}, u32[]{:S(2)}) async-start(bf16[8,1,64,288]{3,2,1,0:T(8,128)(2,1)} %bitcast.73), calls=%async_computation.6 | async-start | bytes 786432 | tf_op jit(solution)/shard_map/all_to_all | solution.py:102
Sparse Core Ops, SparseCore 0:
  9.6 79.6 all-gather.3
